TPU v7x, 32 devices: a whole 2x2x4 slice. The times are simulated.
32 devices in a mesh: dp: 4 (over y, x), fsdp: 8 (over z, core).
Axes of the slice: x: 2, y: 2, z: 4, core: 2. Of those that a mesh axis runs over, the one named last changes fastest.
Arguments:
- latent: bfloat16 [32, 1024, 320], P(('dp', 'fsdp')), may hold values from -6 to 6
- hint: bfloat16 [32, 1024, 320], P(('dp', 'fsdp')), may hold values from -48 to 48
- timestep: int32 [32], P(('dp', 'fsdp')), may hold values from 0 to 999
- skip_grad: bfloat16 [32, 1024, 320], P(('dp', 'fsdp')), may hold values from -6 to 6
- frozen_one: bfloat16 [2880, 320], P('fsdp'), may hold values from -0.109375 to 0.109375
- frozen_two: bfloat16 [2880, 320], P('fsdp'), may hold values from -0.109375 to 0.109375
- time_weight: bfloat16 [320, 1280], P('fsdp'), may hold values from -0.3125 to 0.3125
- frozen_emb: bfloat16 [1280, 320], P('fsdp'), may hold values from -0.15625 to 0.15625
- train_one: bfloat16 [2880, 320], P('fsdp'), may hold values from -0.109375 to 0.109375
- train_two: bfloat16 [2880, 320], P('fsdp'), may hold values from -0.109375 to 0.109375
- train_emb: bfloat16 [1280, 320], P('fsdp'), may hold values from -0.15625 to 0.15625
- zero_weight: bfloat16 [320, 320], P('fsdp'), may hold values from -0.3125 to 0.3125
Outputs:
- skip: bfloat16 [32, 1024, 320], P(('dp', 'fsdp'))
- grad_one: float32 [2880, 320], P('fsdp')
- grad_two: float32 [2880, 320], P('fsdp')
- grad_emb: float32 [1280, 320], P('fsdp')
- grad_zero: float32 [320, 320], P('fsdp')
- grad_norm: float32 [], replicated
All inputs are finite; a program needn't handle non-finite values.
Results may differ from a plain program's by a relative error of at most 0.018.
Values may be sent and summed in bfloat16 or wider, within the bound.
No kernel may reach another device: no remote copies, remote signals or barrier semaphores. Data moves between devices by JAX's collectives and lax.ppermute only.
A program may use at most 128 MiB of HBM per device.

v0:
```python
import math
import jax
import jax.numpy as jnp
from jax import lax
from jax.sharding import PartitionSpec as P

COLS = 64
group_count = 32
clip_limit = 1.0


def conv_apply(flat, kernel):
    count, chans = flat.shape
    height = count // COLS
    padded = jnp.pad(flat.reshape(height, COLS, chans), ((1, 1), (1, 1), (0, 0)))
    total = jnp.zeros((count, kernel.shape[1]), jnp.float32)
    for offset in range(9):
        row_off = offset // 3
        col_off = offset % 3
        piece = padded[row_off : row_off + height, col_off : col_off + COLS].reshape(count, chans)
        total = total + jnp.dot(
            piece, kernel[offset * chans : (offset + 1) * chans], preferred_element_type=jnp.float32
        )
    return total


def conv_back(flat, kernel):
    count, chans = flat.shape
    height = count // COLS
    inner = kernel.shape[0] // 9
    padded = jnp.pad(flat.reshape(height, COLS, chans), ((1, 1), (1, 1), (0, 0)))
    total = jnp.zeros((count, inner), jnp.float32)
    for offset in range(9):
        row_off = offset // 3
        col_off = offset % 3
        piece = padded[
            2 - row_off : 2 - row_off + height, 2 - col_off : 2 - col_off + COLS
        ].reshape(count, chans)
        block = kernel[offset * inner : (offset + 1) * inner]
        total = total + lax.dot_general(
            piece, block, (((1,), (1,)), ((), ())), preferred_element_type=jnp.float32
        )
    return total


def conv_grads(flat, upstream):
    count, chans = flat.shape
    height = count // COLS
    padded = jnp.pad(flat.reshape(height, COLS, chans), ((1, 1), (1, 1), (0, 0)))
    blocks = []
    for offset in range(9):
        row_off = offset // 3
        col_off = offset % 3
        piece = padded[row_off : row_off + height, col_off : col_off + COLS].reshape(count, chans)
        blocks.append(
            lax.dot_general(
                piece, upstream, (((0,), (0,)), ((), ())), preferred_element_type=jnp.float32
            )
        )
    return jnp.concatenate(blocks, axis=0)


def group_norm(value):
    count, chans = value.shape
    grouped = value.reshape(count, group_count, chans // group_count)
    center = jnp.mean(grouped, axis=(0, 2), keepdims=True)
    spread = jnp.mean((grouped - center) ** 2, axis=(0, 2), keepdims=True)
    inverse = lax.rsqrt(spread + 1e-05)
    return (((grouped - center) * inverse).reshape(count, chans), inverse)


def norm_back(upstream, normed, inverse):
    count, chans = upstream.shape
    grouped = upstream.reshape(count, group_count, chans // group_count)
    shaped = normed.reshape(count, group_count, chans // group_count)
    first = jnp.mean(grouped, axis=(0, 2), keepdims=True)
    second = jnp.mean(grouped * shaped, axis=(0, 2), keepdims=True)
    return ((grouped - first - shaped * second) * inverse).reshape(count, chans)


def time_embed(timestep, time_weight):
    half = time_weight.shape[0] // 2
    freqs = jnp.exp(-math.log(10000.0) * jnp.arange(half).astype(jnp.float32) / half)
    angles = timestep.astype(jnp.float32)[:, None] * freqs[None, :]
    wave = jnp.concatenate([jnp.cos(angles), jnp.sin(angles)], axis=1).astype(jnp.bfloat16)
    return jax.nn.silu(jnp.dot(wave, time_weight, preferred_element_type=jnp.float32)).astype(
        jnp.bfloat16
    )


def sample_step(latent_one, hint_one, cotangent, emb_one, weights):
    frozen_one, frozen_two, frozen_emb, train_one, train_two, train_emb, zero_weight = weights
    base = latent_one.astype(jnp.float32)
    emb_row = emb_one[None, :]
    fa0 = jax.nn.silu(group_norm(base)[0]).astype(jnp.bfloat16)
    fp1 = conv_apply(fa0, frozen_one) + jnp.dot(
        emb_row, frozen_emb, preferred_element_type=jnp.float32
    )
    fa1 = jax.nn.silu(group_norm(fp1)[0]).astype(jnp.bfloat16)
    frozen_out = base + conv_apply(fa1, frozen_two)
    mixed_in = base + hint_one.astype(jnp.float32)
    a_zero = jax.nn.silu(group_norm(mixed_in)[0]).astype(jnp.bfloat16)
    p_one = conv_apply(a_zero, train_one) + jnp.dot(
        emb_row, train_emb, preferred_element_type=jnp.float32
    )
    y_one, inverse = group_norm(p_one)
    a_one = jax.nn.silu(y_one).astype(jnp.bfloat16)
    control = (mixed_in + conv_apply(a_one, train_two)).astype(jnp.bfloat16)
    skip_one = (
        frozen_out + jnp.dot(control, zero_weight, preferred_element_type=jnp.float32)
    ).astype(jnp.bfloat16)
    grad_z = lax.dot_general(
        control, cotangent, (((0,), (0,)), ((), ())), preferred_element_type=jnp.float32
    )
    d_control = lax.dot_general(
        cotangent, zero_weight, (((1,), (1,)), ((), ())), preferred_element_type=jnp.float32
    ).astype(jnp.bfloat16)
    grad_w2 = conv_grads(a_one, d_control)
    d_aone = conv_back(d_control, train_two)
    sig = jax.nn.sigmoid(y_one)
    d_yone = d_aone * sig * (1.0 + y_one * (1.0 - sig))
    d_pone = norm_back(d_yone, y_one, inverse)
    grad_e = emb_one.astype(jnp.float32)[:, None] * jnp.sum(d_pone, axis=0)[None, :]
    grad_w1 = conv_grads(a_zero, d_pone.astype(jnp.bfloat16))
    return (skip_one, (grad_w1, grad_w2, grad_e, grad_z))


def run_batch(latent, hint, skip_grad, emb, weights):
    train_one, train_emb, zero_weight = (weights[3], weights[5], weights[6])
    start = (
        jnp.zeros(train_one.shape, jnp.float32),
        jnp.zeros(train_one.shape, jnp.float32),
        jnp.zeros(train_emb.shape, jnp.float32),
        jnp.zeros(zero_weight.shape, jnp.float32),
    )

    def advance(carry, items):
        skip_one, grads = sample_step(items[0], items[1], items[2], items[3], weights)
        return (tuple((old + new for old, new in zip(carry, grads))), skip_one)

    grads, skips = lax.scan(advance, start, (latent, hint, skip_grad, emb))
    return (skips, grads)


def take_rows(whole, shards):
    rows = whole.shape[0] // shards
    return lax.dynamic_slice_in_dim(whole, lax.axis_index("fsdp") * rows, rows, 0)


def body(
    latent,
    hint,
    timestep,
    skip_grad,
    frozen_one,
    frozen_two,
    time_weight,
    frozen_emb,
    train_one,
    train_two,
    train_emb,
    zero_weight,
):
    frozen_full = (
        lax.all_gather(frozen_one, "fsdp", axis=0, tiled=True),
        lax.all_gather(frozen_two, "fsdp", axis=0, tiled=True),
        lax.all_gather(time_weight, "fsdp", axis=0, tiled=True),
        lax.all_gather(frozen_emb, "fsdp", axis=0, tiled=True),
    )
    train_full = (
        lax.all_gather(train_one, "fsdp", axis=0, tiled=True),
        lax.all_gather(train_two, "fsdp", axis=0, tiled=True),
        lax.all_gather(train_emb, "fsdp", axis=0, tiled=True),
        lax.all_gather(zero_weight, "fsdp", axis=0, tiled=True),
    )
    emb = time_embed(timestep, frozen_full[2])
    weights = (
        frozen_full[0],
        frozen_full[1],
        frozen_full[3],
        train_full[0],
        train_full[1],
        train_full[2],
        train_full[3],
    )
    skips, grads = run_batch(latent, hint, skip_grad, emb, weights)
    summed = lax.psum((grads[0], grads[1], grads[2], grads[3]), ("dp", "fsdp"))
    shards = lax.axis_size("fsdp")
    owned = tuple((take_rows(item, shards) for item in summed))
    local_sum = sum((jnp.sum(item * item) for item in owned))
    total = lax.psum(local_sum, "fsdp")
    grad_norm = jnp.sqrt(total + 1e-06)
    scale = jnp.minimum(1.0, clip_limit / grad_norm)
    return (
        skips,
        owned[0] * scale,
        owned[1] * scale,
        owned[2] * scale,
        owned[3] * scale,
        grad_norm,
    )


def solution(mesh):
    in_specs = (
        P(("dp", "fsdp"), None, None),
        P(("dp", "fsdp"), None, None),
        P(("dp", "fsdp")),
        P(("dp", "fsdp"), None, None),
        P("fsdp", None),
        P("fsdp", None),
        P("fsdp", None),
        P("fsdp", None),
        P("fsdp", None),
        P("fsdp", None),
        P("fsdp", None),
        P("fsdp", None),
    )
    out_specs = (
        P(("dp", "fsdp"), None, None),
        P("fsdp", None),
        P("fsdp", None),
        P("fsdp", None),
        P("fsdp", None),
        P(),
    )
    return jax.shard_map(body, mesh=mesh, in_specs=in_specs, out_specs=out_specs, check_vma=False)
```

profile of v0, /device:TPU:0, one launch (start us, length us, event | category | flops | bytes accessed | tf_op | source)
XLA Modules:
  0.0 468.8 jit_solution(11508228289172715350)
XLA Ops:
  14.0 22.5 %all_gather.25 = bf16[320,1280]{1,0:T(8,128)(2,1)S(1)} all-gather(bf16[40,1280]{1,0:T(8,128)(2,1)S(1)} %copy-done.51), channel_id=1, replica_groups=mesh['dp'=4,'fsdp'=8] {'fsdp'}, dimensions={0}, use_global_device_ids=true | all-gather | bytes 921600 | tf_op jit(solution)/shard_map/all_gather | solution.py:167
  36.7 18.6 %all_gather.26 = bf16[1280,320]{1,0:T(8,128)(2,1)S(1)} all-gather(bf16[160,320]{1,0:T(8,128)(2,1)S(1)} %copy-done.49), channel_id=1, replica_groups=mesh['dp'=4,'fsdp'=8] {'fsdp'}, dimensions={0}, use_global_device_ids=true | all-gather | bytes 921600 | tf_op jit(solution)/shard_map/all_gather | solution.py:168
  57.9 22.0 %all_gather.29 = bf16[1280,320]{1,0:T(8,128)(2,1)S(1)} all-gather(bf16[160,320]{1,0:T(8,128)(2,1)S(1)} %copy-done.50), channel_id=1, replica_groups=mesh['dp'=4,'fsdp'=8] {'fsdp'}, dimensions={0}, use_global_device_ids=true | all-gather | bytes 921600 | tf_op jit(solution)/shard_map/all_gather | solution.py:173
  81.8 14.2 %all_gather.31 = bf16[320,320]{1,0:T(8,128)(2,1)S(1)} all-gather(bf16[40,320]{1,0:T(8,128)(2,1)S(1)} %copy-done.52), channel_id=1, replica_groups=mesh['dp'=4,'fsdp'=8] {'fsdp'}, dimensions={0}, use_global_device_ids=true | all-gather | bytes 230400 | tf_op jit(solution)/shard_map/all_gather | solution.py:174
  97.6 3.7 pad_slice_fusion
  101.3 2.9 multiply_convert_fusion
  104.2 6.1 %pad_slice_fusion.16 = (bf16[16,64,320]{2,1,0:T(8,128)(2,1)}, bf16[16,64,320]{2,1,0:T(8,128)(2,1)}, bf16[16,64,320]{2,1,0:T(8,128)(2,1)}, bf16[16,64,320]{2,1,0:...) fusion(bf16[16,64,320]{2,1,0:T(8,128)(2,1)S(1)} %get-tuple-elem, ...), kind=kLoop, calls=%fused_computation.98 | loop fusion | bytes 11796480 | tf_op jit(solution)/shard_map/while/body/eval_jaxpr/slice | solution.py:20
  110.3 4.4 copy.32
  114.7 4.4 reshape.466
  119.1 1.9 fusion.39
  132.6 4.1 copy.34
  136.7 4.6 reshape.468
  141.4 1.9 fusion.96
  151.1 2.1 fusion.101
  154.0 2.6 fusion.103
  169.6 6.2 %pad_slice_fusion.8 = (bf16[16,64,320]{2,1,0:T(8,128)(2,1)S(1)}, bf16[16,64,320]{2,1,0:T(8,128)(2,1)S(1)}, bf16[16,64,320]{2,1,0:T(8,128)(2,1)S(1)}, bf16[16,64,...) fusion(bf16[16,64,320]{2,1,0:T(8,128)(2,1)} %bitcast.244), kind=kLoop, calls=%fused_computation.90 | loop fusion | bytes 5898240 | tf_op jit(solution)/shard_map/while/body/eval_jaxpr/slice | solution.py:54
  193.2 4.1 copy.28
  197.3 4.5 reshape.462
  201.7 4.9 %concatenate.16 = f32[2880,320]{0,1:T(8,128)} concatenate(f32[320,320]{0,1:T(8,128)} %fusion.108, f32[320,320]{0,1:T(8,128)} %fusion.109, f32[320,320]{0,1:T(8,128)} %fusion.110, f32[320,320]{0,1:T(8,128)} %fusion.111, f32[320,320]{0,1:T(8,128)S(1)} %copy-done.46, f32[320,320]{0,1:T(8,128)} %fusion.112, f32[320,320]{0,1:T(8,128)} %fusion.113, f32[320,320]{0,1:T(8,128)} %fusion.114, ...), dimensions={0} | concatenate | bytes 7372800 | tf_op jit(solution)/shard_map/while/body/eval_jaxpr/concatenate | solution.py:60
  206.7 5.1 %concatenate.17 = f32[2880,320]{0,1:T(8,128)} concatenate(f32[320,320]{0,1:T(8,128)} %fusion.116, f32[320,320]{0,1:T(8,128)} %fusion.117, f32[320,320]{0,1:T(8,128)} %fusion.118, f32[320,320]{0,1:T(8,128)} %fusion.119, f32[320,320]{0,1:T(8,128)S(1)} %copy-done.47, f32[320,320]{0,1:T(8,128)} %fusion.120, f32[320,320]{0,1:T(8,128)} %fusion.121, f32[320,320]{0,1:T(8,128)} %fusion.122, ...), dimensions={0} | concatenate | bytes 7372800 | tf_op jit(solution)/shard_map/while/body/eval_jaxpr/concatenate | solution.py:60
  211.8 2.1 fusion.19
  225.7 3.0 fusion.11
  233.2 4.1 copy.30
  237.3 3.4 reshape.464
  240.7 5.9 %pad_slice_fusion.24 = (bf16[16,64,320]{2,1,0:T(8,128)(2,1)S(1)}, bf16[16,64,320]{2,1,0:T(8,128)(2,1)S(1)}, bf16[16,64,320]{2,1,0:T(8,128)(2,1)S(1)}, bf16[16,64...) fusion(bf16[16,64,320]{2,1,0:T(8,128)(2,1)} %bitcast.238), kind=kLoop, calls=%fused_computation.106 | loop fusion | bytes 5898240 | tf_op jit(solution)/shard_map/while/body/eval_jaxpr/slice | solution.py:20
  253.2 171.9 %all-reduce.8.cloned.1.call-done = (f32[2880,320]{0,1:T(8,128)}, f32[2880,320]{0,1:T(8,128)}, f32[1280,320]{1,0:T(8,128)}, f32[320,320]{1,0:T(8,128)}) async-done(((f32[2880,320]{0,1:T(8,128)}, f32[2880,320]{0,1:T(8,128)}, f32[1280,320]{1,0:T(8,128)}, f32[320,320]{1,0:T(8,128)}), (f32[2880,320]{0,1:T(8,128)}, f32[2880,320]{0,1:T(8,128)}, f32[1280,320]{1,0:T(8,128)}, ...) | async-done | bytes 9420816 | tf_op jit(solution)/shard_map/psum | solution.py:187
  425.1 1.9 multiply_reduce_fusion.5
  427.0 1.9 multiply_reduce_fusion.4
  434.6 2.7 fusion.29
  437.3 15.6 %psum.39 = f32[]{:T(128)} all-reduce(f32[]{:T(128)S(6)} %add.398), channel_id=1, replica_groups=mesh['dp'=4,'fsdp'=8] {'fsdp'}, use_global_device_ids=true, to_apply=%region_29.30 | all-reduce | flops 1 | bytes 8 | tf_op jit(solution)/shard_map/psum | solution.py:191
  453.6 2.1 dynamic-slice_multiply_fusion.1
  455.7 2.1 dynamic-slice_multiply_fusion
  (255 shorter events, 91.5 us)
Async XLA Ops:
  7.2 89.5 %copy-start = (bf16[1,1024,320]{1,2,0:T(8,128)(2,1)S(1)}, bf16[1,1024,320]{1,2,0:T(8,128)(2,1)}, u32[]{:S(2)}) copy-start(bf16[1,1024,320]{1,2,0:T(8,128)(2,1)} %param.15) | copy-start | bytes 1966084
  7.2 2.9 copy-start.1
  7.2 103.1 %all-gather.13.cloned.1.call-start = ((), (), s32[]{:S(2)}) async-start(), calls=%async_computation.2 | async-start | bytes 2211840 | tf_op jit(solution)/shard_map/all_gather | solution.py:171
  7.9 124.7 %all-gather.15.cloned.1.call-start = ((), (), s32[]{:S(2)}) async-start(), calls=%async_computation.3 | async-start | bytes 2211840 | tf_op jit(solution)/shard_map/all_gather | solution.py:172
  8.7 184.5 %all-gather.9.cloned.1.call-start = ((), (), s32[]{:S(2)}) async-start(), calls=%async_computation | async-start | bytes 2211840 | tf_op jit(solution)/shard_map/all_gather | solution.py:165
  8.7 2.8 copy-start.4
  9.4 223.8 %all-gather.11.cloned.1.call-start = ((), (), s32[]{:S(2)}) async-start(), calls=%async_computation.1 | async-start | bytes 2211840 | tf_op jit(solution)/shard_map/all_gather | solution.py:166
  10.0 415.1 %all-reduce.8.cloned.1.call-start = ((), (), s32[]{:S(2)}) async-start(), calls=%async_computation.4 | async-start | bytes 19988480 | tf_op jit(solution)/shard_map/psum | solution.py:187
  11.5 2.5 copy-start.51
  12.9 23.8 %copy-start.49 = (bf16[160,320]{1,0:T(8,128)(2,1)S(1)}, bf16[160,320]{1,0:T(8,128)(2,1)}, u32[]{:S(2)}) copy-start(bf16[160,320]{1,0:T(8,128)(2,1)} %param.19) | copy-start | bytes 307204
  55.3 2.5 copy-start.50
  80.1 1.7 copy-start.52
  110.3 15.9 %copy-start.8 = (bf16[16,64,320]{2,1,0:T(8,128)(2,1)}, bf16[16,64,320]{2,1,0:T(8,128)(2,1)S(1)}, u32[]{:S(2)}) copy-start(bf16[16,64,320]{2,1,0:T(8,128)(2,1)S(1)} %get-tuple-element.91) | copy-start | bytes 1966084
  119.1 1.9 copy-start.6
  121.0 1.8 copy-start.18
  136.7 6.5 %copy-start.38 = (bf16[16,64,320]{2,1,0:T(8,128)(2,1)S(1)}, bf16[16,64,320]{2,1,0:T(8,128)(2,1)}, u32[]{:S(2)}) copy-start(bf16[16,64,320]{2,1,0:T(8,128)(2,1)} %get-tuple-element.73) | copy-start | bytes 1966084
  141.3 1.9 copy-start.2
  149.6 1.5 copy-start.48
  154.0 2.6 copy-start.21
  169.6 6.2 %copy-start.3 = (bf16[2880,320]{0,1:T(8,128)(2,1)S(1)}, bf16[2880,320]{0,1:T(8,128)(2,1)}, u32[]{:S(2)}) copy-start(bf16[2880,320]{0,1:T(8,128)(2,1)} %reshape.468) | copy-start | bytes 5529604
  175.8 13.0 %copy-start.22 = (bf16[16,64,320]{2,1,0:T(8,128)(2,1)}, bf16[16,64,320]{2,1,0:T(8,128)(2,1)S(1)}, u32[]{:S(2)}) copy-start(bf16[16,64,320]{2,1,0:T(8,128)(2,1)S(1)} %get-tuple-element.80) | copy-start | bytes 1966084
  197.3 4.5 copy-start.46
  201.7 4.9 %copy-start.47 = (f32[320,320]{0,1:T(8,128)S(1)}, f32[320,320]{0,1:T(8,128)}, u32[]{:S(2)}) copy-start(f32[320,320]{0,1:T(8,128)} %fusion.107) | copy-start | bytes 1228804
  206.7 5.1 %copy-start.23 = (bf16[16,64,320]{2,1,0:T(8,128)(2,1)S(1)}, bf16[16,64,320]{2,1,0:T(8,128)(2,1)}, u32[]{:S(2)}) copy-start(bf16[16,64,320]{2,1,0:T(8,128)(2,1)} %copy-done.22) | copy-start | bytes 1966084
  211.8 3.5 copy-start.7
  213.9 3.0 copy-start.28
  215.3 1.7 copy-start.42
  216.9 1.6 copy-start.41
  218.5 1.7 copy-start.40
  225.7 3.1 copy-start.39
  253.2 181.3 %copy-start.29 = (bf16[1024,320]{0,1:T(8,128)(2,1)S(1)}, bf16[1024,320]{0,1:T(8,128)(2,1)}, u32[]{:S(2)}) copy-start(bf16[1024,320]{0,1:T(8,128)(2,1)} %copy-done.28) | copy-start | bytes 1966084
  253.2 181.3 %copy-start.45 = (bf16[320,320]{1,0:T(8,128)(2,1)S(1)}, bf16[320,320]{1,0:T(8,128)(2,1)}, u32[]{:S(2)}) copy-start(bf16[320,320]{1,0:T(8,128)(2,1)} %copy-done.44) | copy-start | bytes 614404
  (26 other events, 30.9 us)
Sparse Core Ops, SparseCore 0:
  9.6 37.1 all-gather.12
  48.5 36.0 all-gather.14
  86.2 27.3 all-gather.8
  115.2 27.4 all-gather.10
  225.9 199.1 all-reduce.7
where the time goes:
time: 476 us; the launch traced here: 469 us
  waiting for transfers between devices  175 us (37%)
  blocking collectives  92.9 us (20%)
  local copies, waits for them, and re-layouts  83.1 us (17%)
  matrix products  70.8 us (15%)
  other arithmetic  27.4 us (6%)
  between operations  20 us (4%)
    psum x1, waiting for transfers between devices, body(): summed = lax.psum((grads[0], grads[1], grads[2], grads[3]), ('dp', 'fsdp'))  172 us
    dot_general x36, matrix products, conv_apply(): jnp.dot(piece, kernel[offset * chans:(offset + 1) * chans], preferred_ele...  33.7 us
    unnamed x110, local copies, waits for them, and re-layouts  26 us
    dot_general x18, matrix products, conv_grads(): lax.dot_general(piece, upstream, (((0,), (0,)), ((), ())), preferred_elem...  23.7 us
    all_gather x1, blocking collectives, body(): lax.all_gather(time_weight, 'fsdp', axis=0, tiled=True)  22.5 us
    all_gather x1, blocking collectives, body(): lax.all_gather(train_emb, 'fsdp', axis=0, tiled=True)  22 us
    all_gather x1, blocking collectives, body(): lax.all_gather(frozen_emb, 'fsdp', axis=0, tiled=True)  18.6 us
    psum x1, blocking collectives, body(): total = lax.psum(local_sum, 'fsdp')  15.6 us
  transfers between devices with their start and end apart: 5, of which 1 were waited for; matrix products, arithmetic and copies ran while one was open for 33% of the time, Pallas kernels for 0%

commit v1 on v0

--- a/solution.py
+++ b/solution.py
@@ -1,3 +1,4 @@
+import functools
 import math
 import jax
 import jax.numpy as jnp
@@ -7,6 +8,14 @@
 COLS = 64
 group_count = 32
 clip_limit = 1.0
+
+
+def connect_task(xin, row_axis, mesh_ax):
+    u1 = lax.psum(lax.psum(xin, row_axis), mesh_ax)
+    return u1
+
+
+move_thing = functools.partial(connect_task, row_axis="fsdp", mesh_ax="dp")
 
 
 def conv_apply(flat, kernel):
@@ -184,7 +193,7 @@
         train_full[3],
     )
     skips, grads = run_batch(latent, hint, skip_grad, emb, weights)
-    summed = lax.psum((grads[0], grads[1], grads[2], grads[3]), ("dp", "fsdp"))
+    summed = move_thing((grads[0], grads[1], grads[2], grads[3]))
     shards = lax.axis_size("fsdp")
     owned = tuple((take_rows(item, shards) for item in summed))
     local_sum = sum((jnp.sum(item * item) for item in owned))

time: 476 us -> 701 us (1.47)
  waiting for transfers between devices: 175 us -> 409 us
    psum x1 -> x2, waiting for transfers between devices: 172 us -> 386 us  [connect_task(): u1 = lax.psum(lax.psum(xin, row_axis), mesh_ax)]
    all_gather x1, waiting for transfers between devices: 0.01 us -> 12.5 us  [body(): lax.all_gather(frozen_one, 'fsdp', axis=0, tiled=True)]
    all_gather x1, waiting for transfers between devices: 0.01 us -> 7.94 us  [body(): lax.all_gather(frozen_two, 'fsdp', axis=0, tiled=True)]
    unnamed x110 -> x114, local copies, waits for them, and re-layouts: 26 us -> 28 us
  transfers between devices with their start and end apart: 5 -> 6, of which waited for: 1 -> 4; matrix products, arithmetic and copies ran while one was open for 33% -> 11% of each run, Pallas kernels for 0% -> 0%
where the time goes in v1:
time: 701 us; the launch traced here: 694 us
  waiting for transfers between devices  409 us (58%)
  blocking collectives  89.9 us (13%)
  local copies, waits for them, and re-layouts  84.7 us (12%)
  matrix products  64.4 us (9%)
  other arithmetic  25.4 us (4%)
  between operations  20.4 us (3%)
    psum x2, waiting for transfers between devices, connect_task(): u1 = lax.psum(lax.psum(xin, row_axis), mesh_ax)  386 us
    unnamed x114, local copies, waits for them, and re-layouts  28 us
    dot_general x36, matrix products, conv_apply(): jnp.dot(piece, kernel[offset * chans:(offset + 1) * chans], preferred_ele...  27.4 us
    dot_general x18, matrix products, conv_grads(): lax.dot_general(piece, upstream, (((0,), (0,)), ((), ())), preferred_elem...  23.6 us
    all_gather x1, blocking collectives, body(): lax.all_gather(time_weight, 'fsdp', axis=0, tiled=True)  22.5 us
    all_gather x1, blocking collectives, body(): lax.all_gather(frozen_emb, 'fsdp', axis=0, tiled=True)  17.8 us
    all_gather x1, blocking collectives, body(): lax.all_gather(train_emb, 'fsdp', axis=0, tiled=True)  17.5 us
    psum x1, blocking collectives, body(): total = lax.psum(local_sum, 'fsdp')  16.7 us
  transfers between devices with their start and end apart: 6, of which 4 were waited for; matrix products, arithmetic and copies ran while one was open for 11% of the time, Pallas kernels for 0%

profile of v1, /device:TPU:0, one launch (start us, length us, event | category | flops | bytes accessed | tf_op | source)
XLA Modules:
  0.0 694.3 jit_solution(11702591857733900415)
XLA Ops:
  8.7 2.5 copy.27
  13.8 22.5 %all_gather.25 = bf16[320,1280]{1,0:T(8,128)(2,1)S(1)} all-gather(bf16[40,1280]{1,0:T(8,128)(2,1)S(1)} %copy-done.53), channel_id=1, replica_groups=mesh['dp'=4,'fsdp'=8] {'fsdp'}, dimensions={0}, use_global_device_ids=true | all-gather | bytes 921600 | tf_op jit(solution)/shard_map/all_gather | solution.py:176
  39.1 17.5 %all_gather.29 = bf16[1280,320]{1,0:T(8,128)(2,1)} all-gather(bf16[160,320]{1,0:T(8,128)(2,1)S(1)} %copy-done.51), channel_id=1, replica_groups=mesh['dp'=4,'fsdp'=8] {'fsdp'}, dimensions={0}, use_global_device_ids=true | all-gather | bytes 921600 | tf_op jit(solution)/shard_map/all_gather | solution.py:182
  58.1 15.4 %all_gather.31 = bf16[320,320]{1,0:T(8,128)(2,1)S(1)} all-gather(bf16[40,320]{1,0:T(8,128)(2,1)S(1)} %copy-done.54), channel_id=1, replica_groups=mesh['dp'=4,'fsdp'=8] {'fsdp'}, dimensions={0}, use_global_device_ids=true | all-gather | bytes 230400 | tf_op jit(solution)/shard_map/all_gather | solution.py:183
  75.0 3.7 pad_slice_fusion
  79.7 6.0 pad_slice_fusion.16
  86.0 4.0 copy.32
  90.0 4.4 reshape.466
  107.9 4.0 copy.34
  111.9 4.6 reshape.468
  126.2 2.1 fusion.101
  129.1 2.6 fusion.103
  144.6 6.1 pad_slice_fusion.8
  171.5 4.8 concatenate.16
  176.3 4.9 concatenate.17
  182.4 204.8 %all-reduce.10.cloned.1.call-done = (f32[2880,320]{0,1:T(8,128)}, f32[2880,320]{0,1:T(8,128)}, f32[1280,320]{1,0:T(8,128)}, f32[320,320]{1,0:T(8,128)}) async-done(((f32[2880,320]{0,1:T(8,128)}, f32[2880,320]{0,1:T(8,128)}, f32[1280,320]{1,0:T(8,128)}, f32[320,320]{1,0:T(8,128)}), (f32[2880,320]{0,1:T(8,128)}, f32[2880,320]{0,1:T(8,128)}, f32[1280,320]{1,0:T(8,128)}, ...) | async-done | bytes 9420816 | tf_op jit(solution)/shard_map/psum | solution.py:14
  388.2 17.8 %all_gather.26 = bf16[1280,320]{1,0:T(8,128)(2,1)S(1)} all-gather(bf16[160,320]{1,0:T(8,128)(2,1)S(1)} %copy-done.52), channel_id=1, replica_groups=mesh['dp'=4,'fsdp'=8] {'fsdp'}, dimensions={0}, use_global_device_ids=true | all-gather | bytes 921600 | tf_op jit(solution)/shard_map/all_gather | solution.py:177
  406.3 12.5 %all-gather.9.cloned.1.call-done = bf16[8,360,320]{1,2,0:T(8,128)(2,1)} async-done(((bf16[1,360,320]{1,2,0:T(8,128)(2,1)}), bf16[8,360,320]{1,2,0:T(8,128)(2,1)}) %all-gather.9.cloned.1.call-update) | async-done | bytes 1843216 | tf_op jit(solution)/shard_map/all_gather | solution.py:174
  418.8 4.0 copy.28
  422.7 3.5 reshape.462
  426.3 2.3 fusion.65
  439.9 7.9 %all-gather.11.cloned.1.call-done = bf16[8,360,320]{1,2,0:T(8,128)(2,1)} async-done(((bf16[1,360,320]{1,2,0:T(8,128)(2,1)}), bf16[8,360,320]{1,2,0:T(8,128)(2,1)}) %all-gather.11.cloned.1.call-update) | async-done | bytes 1843216 | tf_op jit(solution)/shard_map/all_gather | solution.py:175
  447.9 4.0 copy.30
  451.9 3.4 reshape.464
  455.2 5.9 pad_slice_fusion.24
  467.8 181.4 %all-reduce.12.cloned.1.call-done = (f32[2880,320]{0,1:T(8,128)}, f32[2880,320]{0,1:T(8,128)}, f32[1280,320]{1,0:T(8,128)}, f32[320,320]{1,0:T(8,128)}) async-done(((f32[2880,320]{0,1:T(8,128)}, f32[2880,320]{0,1:T(8,128)}, f32[1280,320]{1,0:T(8,128)}, f32[320,320]{1,0:T(8,128)}), (f32[2880,320]{0,1:T(8,128)}, f32[2880,320]{0,1:T(8,128)}, f32[1280,320]{1,0:T(8,128)}, ...) | async-done | bytes 9420816 | tf_op jit(solution)/shard_map/psum | solution.py:14
  649.2 1.9 multiply_reduce_fusion.5
  651.1 1.9 multiply_reduce_fusion.4
  658.7 2.7 fusion.29
  661.4 16.7 %psum.71 = f32[]{:T(128)} all-reduce(f32[]{:T(128)S(6)} %add.406), channel_id=1, replica_groups=mesh['dp'=4,'fsdp'=8] {'fsdp'}, use_global_device_ids=true, to_apply=%region_33.34 | all-reduce | flops 1 | bytes 8 | tf_op jit(solution)/shard_map/psum | solution.py:200
  678.8 2.1 dynamic-slice_multiply_fusion.1
  680.9 2.1 dynamic-slice_multiply_fusion
  (262 shorter events, 94.0 us)
Async XLA Ops:
  7.2 67.0 %copy-start = (bf16[1,1024,320]{1,2,0:T(8,128)(2,1)S(1)}, bf16[1,1024,320]{1,2,0:T(8,128)(2,1)}, u32[]{:S(2)}) copy-start(bf16[1,1024,320]{1,2,0:T(8,128)(2,1)} %param.15) | copy-start | bytes 1966084
  7.2 78.9 %all-gather.13.cloned.1.call-start = ((), (), s32[]{:S(2)}) async-start(), calls=%async_computation.2 | async-start | bytes 2211840 | tf_op jit(solution)/shard_map/all_gather | solution.py:180
  7.2 4.0 copy-start.4
  7.9 100.0 %all-gather.15.cloned.1.call-start = ((), (), s32[]{:S(2)}) async-start(), calls=%async_computation.3 | async-start | bytes 2211840 | tf_op jit(solution)/shard_map/all_gather | solution.py:181
  8.7 378.6 %all-reduce.10.cloned.1.call-start = ((), (), s32[]{:S(2)}) async-start(), calls=%async_computation.4 | async-start | bytes 19988480 | tf_op jit(solution)/shard_map/psum | solution.py:14
  11.2 1.5 copy-start.1
  11.2 2.5 copy-start.53
  36.5 2.6 copy-start.51
  39.1 18.9 %copy-start.54 = (bf16[40,320]{1,0:T(8,128)(2,1)S(1)}, bf16[40,320]{1,0:T(8,128)(2,1)}, u32[]{:S(2)}) copy-start(bf16[40,320]{1,0:T(8,128)(2,1)} %param.23) | copy-start | bytes 76804
  75.0 3.7 copy-start.22
  75.0 3.7 copy-start.23
  79.7 6.0 copy-start.30
  85.7 15.8 %copy-start.8 = (bf16[16,64,320]{2,1,0:T(8,128)(2,1)}, bf16[16,64,320]{2,1,0:T(8,128)(2,1)S(1)}, u32[]{:S(2)}) copy-start(bf16[16,64,320]{2,1,0:T(8,128)(2,1)S(1)} %get-tuple-element.95) | copy-start | bytes 1966084
  94.4 1.9 copy-start.6
  96.3 1.8 copy-start.18
  111.9 6.5 copy-start.39
  116.4 1.9 copy-start.2
  124.6 1.5 copy-start.50
  129.1 2.6 copy-start.21
  144.6 6.1 copy-start.3
  169.7 1.6 copy-start.46
  169.7 1.6 copy-start.48
  169.7 1.8 copy-start.49
  171.5 4.8 copy-start.47
  181.2 237.5 %all-gather.9.cloned.1.call-start = ((), (), s32[]{:S(2)}) async-start(), calls=%async_computation | async-start | bytes 2211840 | tf_op jit(solution)/shard_map/all_gather | solution.py:174
  181.8 266.1 %all-gather.11.cloned.1.call-start = ((), (), s32[]{:S(2)}) async-start(), calls=%async_computation.1 | async-start | bytes 2211840 | tf_op jit(solution)/shard_map/all_gather | solution.py:175
  182.4 466.9 %all-reduce.12.cloned.1.call-start = ((), (), s32[]{:S(2)}) async-start(), calls=%async_computation.5 | async-start | bytes 19988480 | tf_op jit(solution)/shard_map/psum | solution.py:14
  426.3 8.0 %copy-start.7 = (bf16[2880,320]{0,1:T(8,128)(2,1)}, bf16[2880,320]{0,1:T(8,128)(2,1)S(1)}, u32[]{:S(2)}) copy-start(bf16[2880,320]{0,1:T(8,128)(2,1)S(1)} %reshape.462) | copy-start | bytes 5529604
  426.3 2.4 copy-start.43
  438.7 9.1 %copy-start.26 = (bf16[1024,320]{0,1:T(8,128)(2,1)}, bf16[1024,320]{0,1:T(8,128)(2,1)S(1)}, u32[]{:S(2)}) copy-start(bf16[1024,320]{0,1:T(8,128)(2,1)S(1)} %multiply_convert_fusion.4) | copy-start | bytes 1966084
  467.8 190.9 %copy-start.29 = (bf16[1024,320]{0,1:T(8,128)(2,1)S(1)}, bf16[1024,320]{0,1:T(8,128)(2,1)}, u32[]{:S(2)}) copy-start(bf16[1024,320]{0,1:T(8,128)(2,1)} %copy-done.28) | copy-start | bytes 1966084
  467.8 190.9 %copy-start.45 = (bf16[320,320]{1,0:T(8,128)(2,1)S(1)}, bf16[320,320]{1,0:T(8,128)(2,1)}, u32[]{:S(2)}) copy-start(bf16[320,320]{1,0:T(8,128)(2,1)} %copy-done.44) | copy-start | bytes 614404
  (29 other events, 33.8 us)
Sparse Core Ops, SparseCore 0:
  9.6 34.8 all-gather.12
  46.2 30.3 all-gather.14
  181.3 205.8 all-reduce.9
  388.8 29.9 all-gather.8
  420.2 27.5 all-gather.10
  451.7 197.4 all-reduce.11
